TPU v7x, 32 devices: a whole 2x2x4 slice. The times are simulated.
32 devices in a mesh: batch: 4 (over x, core), space: 8 (over z, y).
Axes of the slice: x: 2, y: 2, z: 4, core: 2. Of those that a mesh axis runs over, the one named last changes fastest.
Arguments:
- inputs: bfloat16 [4, 128, 64, 64, 128], P('batch', 'space'), may hold values from -6 to 6
- cotangent: bfloat16 [4, 128, 64, 64, 128], P('batch', 'space'), may hold values from -6 to 6
- mode_weights: bfloat16 [256, 16, 64, 128], P('space'), may hold values from -1.5 to 1.5
Outputs:
- input_grad: bfloat16 [4, 128, 64, 64, 128], P('batch', 'space')
- weight_grad: float32 [256, 16, 64, 128], P('space')
All inputs are finite; a program needn't handle non-finite values.
Results may differ from a plain program's by a relative error of at most 0.015.
Values may be sent and summed in bfloat16 or wider, within the bound.
No kernel may reach another device: no remote copies, remote signals or barrier semaphores. Data moves between devices by JAX's collectives and lax.ppermute only.
A program may use at most 192 MiB of HBM per device.

v0:
```python
import math
import jax
import jax.numpy as jnp
from jax import lax
from jax.sharding import PartitionSpec as P

C = 64
X = 64
Y = 128
Z = 128
MX = 16
MY = 16
MZ = 16
two_pi = 2.0 * math.pi
highest = lax.Precision.HIGHEST


def twiddles(wave_list, positions, length):
    product = wave_list[:, None] * positions[None, :] % length
    angles = two_pi / length * product.astype(jnp.float32)
    return (jnp.cos(angles), jnp.sin(angles))


def wave_pair(retained, length):
    return jnp.concatenate([jnp.arange(retained // 2), jnp.arange(length - retained // 2, length)])


def plane_spectrum(values, z_table, cos_x, sin_x, factor):
    lead_dims = values.shape[:-3]
    along_z = jnp.dot(values.reshape(-1, Z), z_table, preferred_element_type=jnp.float32)
    along_z = along_z.reshape(lead_dims + (C, X, 2 * MZ))
    first_term = jnp.einsum("kx,...cxm->...ckm", cos_x, along_z, precision=highest)
    second_term = jnp.einsum("kx,...cxm->...ckm", sin_x, along_z, precision=highest)
    real_part = (first_term[..., :MZ] + second_term[..., MZ:]) * factor
    imag_part = (first_term[..., MZ:] - second_term[..., :MZ]) * factor
    stacked = jnp.stack([real_part, imag_part], axis=-4)
    return stacked.reshape(lead_dims + (2, C, MX * MZ)).astype(jnp.bfloat16)


def modes_along_y(spectra, cos_y, sin_y):
    values_f = spectra.astype(jnp.float32)
    real_in = values_f[:, :, 0]
    imag_in = values_f[:, :, 1]
    real_out = jnp.einsum("ky,bycp->pbkc", cos_y, real_in, precision=highest) + jnp.einsum(
        "ky,bycp->pbkc", sin_y, imag_in, precision=highest
    )
    imag_out = jnp.einsum("ky,bycp->pbkc", cos_y, imag_in, precision=highest) - jnp.einsum(
        "ky,bycp->pbkc", sin_y, real_in, precision=highest
    )
    return jnp.stack([real_out, imag_out], axis=3)


def planes_along_y(mode_data, cos_y, sin_y):
    values_f = mode_data.astype(jnp.float32)
    real_in = values_f[:, :, :, 0]
    imag_in = values_f[:, :, :, 1]
    real_out = jnp.einsum("ky,pbkc->bycp", cos_y, real_in, precision=highest) - jnp.einsum(
        "ky,pbkc->bycp", sin_y, imag_in, precision=highest
    )
    imag_out = jnp.einsum("ky,pbkc->bycp", sin_y, real_in, precision=highest) + jnp.einsum(
        "ky,pbkc->bycp", cos_y, imag_in, precision=highest
    )
    return jnp.stack([real_out, imag_out], axis=2)


def plane_inverse(spectra, cos_x, sin_x, z_back):
    lead_dims = spectra.shape[:-3]
    values_f = spectra.astype(jnp.float32).reshape(lead_dims + (2, C, MX, MZ))
    real_in = values_f[..., 0, :, :, :]
    imag_in = values_f[..., 1, :, :, :]
    real_out = jnp.einsum("kx,...ckm->...cxm", cos_x, real_in, precision=highest) - jnp.einsum(
        "kx,...ckm->...cxm", sin_x, imag_in, precision=highest
    )
    imag_out = jnp.einsum("kx,...ckm->...cxm", sin_x, real_in, precision=highest) + jnp.einsum(
        "kx,...ckm->...cxm", cos_x, imag_in, precision=highest
    )
    joined = jnp.concatenate([real_out, imag_out], axis=-1)
    result = jnp.dot(
        joined.reshape(-1, 2 * MZ), z_back, precision=highest, preferred_element_type=jnp.float32
    )
    return result.reshape(lead_dims + (C, X, Z)).astype(jnp.bfloat16)


def split_cot(cot_modes):
    real_part = cot_modes[:, :, :, 0]
    imag_part = cot_modes[:, :, :, 1]
    return (
        jnp.concatenate([real_part, imag_part], axis=-1),
        jnp.concatenate([imag_part, -real_part], axis=-1),
    )


def weight_terms(input_modes, cot_modes):
    cot_one, cot_two = split_cot(cot_modes)
    first_term = jnp.einsum(
        "pbki,pbkj->pkij", input_modes[:, :, :, 0], cot_one, preferred_element_type=jnp.float32
    )
    second_term = jnp.einsum(
        "pbki,pbkj->pkij", input_modes[:, :, :, 1], cot_two, preferred_element_type=jnp.float32
    )
    return first_term + second_term


def local(inputs, cotangent, mode_weights):
    inv_scale = 1.0 / math.sqrt(X * Y * Z)
    cos_z, sin_z = twiddles(jnp.arange(MZ), jnp.arange(Z), Z)
    z_table = jnp.concatenate([cos_z.T, -sin_z.T], axis=1).astype(jnp.bfloat16)
    z_back = jnp.concatenate([cos_z, -sin_z], axis=0) * inv_scale
    cos_x, sin_x = twiddles(wave_pair(MX, X), jnp.arange(X), X)
    plain_z = jnp.full((MZ,), inv_scale, jnp.float32)
    weight_z = jnp.where(jnp.arange(MZ) == 0, 1.0, 2.0).astype(jnp.float32) * inv_scale
    input_spec = plane_spectrum(inputs, z_table, cos_x, sin_x, plain_z)
    cot_spec = plane_spectrum(cotangent, z_table, cos_x, sin_x, weight_z)
    y_waves = wave_pair(MY, Y)
    positions = jnp.arange(Y)
    cos_y, sin_y = twiddles(y_waves, positions, Y)
    moved_input, moved_cot = (
        lax.all_to_all(input_spec, "space", split_axis=4, concat_axis=1, tiled=True),
        lax.all_to_all(cot_spec, "space", split_axis=4, concat_axis=1, tiled=True),
    )
    input_modes = modes_along_y(moved_input, cos_y, sin_y)
    cot_modes = modes_along_y(moved_cot, cos_y, sin_y)
    input_modes = input_modes.astype(jnp.bfloat16)
    cot_modes = cot_modes.astype(jnp.bfloat16)
    weight_grad = lax.psum(
        weight_terms(input_modes, cot_modes).astype(jnp.bfloat16), "batch"
    ).astype(jnp.float32)
    cot_one, cot_two = split_cot(cot_modes)
    grad_real = jnp.einsum(
        "pbkj,pkij->pbki", cot_one, mode_weights, preferred_element_type=jnp.float32
    )
    grad_imag = jnp.einsum(
        "pbkj,pkij->pbki", cot_two, mode_weights, preferred_element_type=jnp.float32
    )
    mode_grad = jnp.stack([grad_real, grad_imag], axis=3).astype(jnp.bfloat16)
    plane_modes = planes_along_y(mode_grad, cos_y, sin_y).astype(jnp.bfloat16)
    back_spec = lax.all_to_all(plane_modes, "space", split_axis=1, concat_axis=4, tiled=True)
    input_grad = plane_inverse(back_spec, cos_x, sin_x, z_back)
    return (input_grad, weight_grad)


def solution(mesh):
    placed = (
        P("batch", "space", None, None, None),
        P("batch", "space", None, None, None),
        P("space", None, None, None),
    )
    return jax.shard_map(
        local,
        mesh=mesh,
        in_specs=placed,
        out_specs=(P("batch", "space", None, None, None), P("space", None, None, None)),
        check_vma=False,
    )
```

profile of v0, /device:TPU:0, one launch (start us, length us, event | category | flops | bytes accessed | tf_op | source)
XLA Modules:
  0.0 509.5 jit_solution(14194246704716014748)
XLA Ops:
  7.2 15.0 %convolution_bitcast_fusion.1 = f32[65536,32]{0,1:T(8,128)} fusion(bf16[65536,128]{1,0:T(8,128)(2,1)} %bitcast.208, bf16[128,16]{0,1:T(8,128)(2,1)S(1)} %get-tuple-element.24, bf16[128,16]{0,1:T(8,128)(2,1)S(1)} %get-tuple-element.25), kind=kOutput, calls=%fused_computation.1 | convolution fusion | flops 536887296 | bytes 25174016 | tf_op jit(solution)/shard_map/dot_general | solution.py:30
  22.3 12.2 %reshape.397 = f32[16,64,64,32]{2,1,0,3:T(8,128)} reshape(f32[65536,32]{0,1:T(8,128)} %convolution_bitcast_fusion.1) | data formatting | bytes 16777216 | tf_op jit(solution)/shard_map/reshape
  34.5 41.9 %fusion.15 = f32[1,16,64,16,32]{2,3,4,1,0:T(8,128)S(1)} fusion(f32[16,64,64,32]{2,1,0,3:T(8,128)} %reshape.397, s32[16]{0:T(128)S(1)} %get-tuple-element.21), kind=kOutput, calls=%fused_computation.18 | convolution fusion | flops 402667520 | bytes 10485824 | tf_op jit(solution)/shard_map/kx,...cxm->...ckm/dot_general | solution.py:33
  76.5 39.9 %fusion.12 = f32[1,16,64,16,32]{2,3,4,1,0:T(8,128)S(1)} fusion(f32[16,64,64,32]{2,1,0,3:T(8,128)S(1)} %copy-done, s32[16]{0:T(128)S(1)} %get-tuple-element.21), kind=kOutput, calls=%fused_computation.17 | convolution fusion | flops 402667520 | bytes 10485824 | tf_op jit(solution)/shard_map/kx,...cxm->...ckm/dot_general | solution.py:32
  122.4 7.3 %all-to-all-start = ((bf16[8,2,32768]{2,1,0:T(2,128)(2,1)}), bf16[8,2,32768]{2,1,0:T(2,128)(2,1)S(1)}, u32[]{:S(2)}, u32[]{:S(2)}) async-start(bf16[8,2,32768]{2,1,0:T(2,128)(2,1)} %reshape.424), calls=%async_computation | async-start | bytes 2097152 | tf_op jit(solution)/shard_map/all_to_all | solution.py:119
  129.7 15.0 %convolution_bitcast_fusion = f32[65536,32]{0,1:T(8,128)} fusion(bf16[65536,128]{1,0:T(8,128)(2,1)} %bitcast.209, bf16[128,16]{0,1:T(8,128)(2,1)S(1)} %get-tuple-element.24, bf16[128,16]{0,1:T(8,128)(2,1)S(1)} %get-tuple-element.25), kind=kOutput, calls=%fused_computation | convolution fusion | flops 536887296 | bytes 25174016 | tf_op jit(solution)/shard_map/dot_general | solution.py:30
  144.7 12.2 %reshape.406 = f32[16,64,64,32]{2,1,0,3:T(8,128)} reshape(f32[65536,32]{0,1:T(8,128)} %convolution_bitcast_fusion) | data formatting | bytes 16777216 | tf_op jit(solution)/shard_map/reshape.48
  157.0 41.9 %fusion.21 = f32[1,16,64,16,32]{2,3,4,1,0:T(8,128)S(1)} fusion(f32[16,64,64,32]{2,1,0,3:T(8,128)} %reshape.406, s32[16]{0:T(128)S(1)} %get-tuple-element.21), kind=kOutput, calls=%fused_computation.20 | convolution fusion | flops 402667520 | bytes 10485824 | tf_op jit(solution)/shard_map/kx,...cxm->...ckm/dot_general | solution.py:33
  198.9 39.6 %fusion.18 = f32[1,16,64,16,32]{2,3,4,1,0:T(8,128)S(1)} fusion(f32[16,64,64,32]{2,1,0,3:T(8,128)S(1)} %copy-done.1, s32[16]{0:T(128)S(1)} %get-tuple-element.21), kind=kOutput, calls=%fused_computation.19 | convolution fusion | flops 402667520 | bytes 10485824 | tf_op jit(solution)/shard_map/kx,...cxm->...ckm/dot_general | solution.py:32
  245.3 6.0 %all-to-all-start.2 = ((bf16[8,2,32768]{2,1,0:T(2,128)(2,1)}), bf16[8,2,32768]{2,1,0:T(2,128)(2,1)S(1)}, u32[]{:S(2)}, u32[]{:S(2)}) async-start(bf16[8,2,32768]{2,1,0:T(2,128)(2,1)} %reshape.428), calls=%async_computation.2 | async-start | bytes 2097152 | tf_op jit(solution)/shard_map/all_to_all | solution.py:118
  258.0 3.6 copy.109
  261.6 3.6 copy.108
  274.5 7.8 %fusion.64 = f32[32,16,1,64]{3,2,1,0:T(1,128)S(1)} fusion(bf16[32,16,64,128]{3,2,1,0:T(8,128)(2,1)} %param.5, bf16[32,16,128,1]{2,1,0,3:T(8,128)(2,1)S(1)} %get-tuple-element.15), kind=kOutput, calls=%fused_computation.76 | convolution fusion | flops 8388608 | bytes 8650752 | tf_op jit(solution)/shard_map/pbkj,pkij->pbki/dot_general | solution.py:129
  283.1 8.2 %fusion.62 = f32[32,16,1,64]{3,2,1,0:T(1,128)S(1)} fusion(bf16[32,16,64,128]{3,2,1,0:T(8,128)(2,1)} %param.5, bf16[32,16,128,1]{2,1,0,3:T(8,128)(2,1)S(1)} %get-tuple-element.18), kind=kOutput, calls=%fused_computation.74 | convolution fusion | flops 8388608 | bytes 8650752 | tf_op jit(solution)/shard_map/pbkj,pkij->pbki/dot_general | solution.py:132
  294.8 3.9 copy.81
  301.4 6.0 %all-to-all-start.1 = ((bf16[8,2,32768]{2,1,0:T(2,128)(2,1)}), bf16[8,2,32768]{2,1,0:T(2,128)(2,1)}, u32[]{:S(2)}, u32[]{:S(2)}) async-start(bf16[8,2,32768]{2,1,0:T(2,128)(2,1)} %reshape.426), calls=%async_computation.1 | async-start | bytes 2097152 | tf_op jit(solution)/shard_map/all_to_all | solution.py:137
  323.4 12.6 %add_convert_fusion = bf16[32,16,64,128]{3,2,1,0:T(8,128)(2,1)} fusion(f32[32,16,128]{2,1,0:T(8,128)} %get-tuple-element.19, f32[32,16,64]{2,1,0:T(8,128)S(1)} %copy.96, f32[32,16,128]{2,1,0:T(8,128)S(1)} %get-tuple-element.14, f32[32,16,64]{2,1,0:T(8,128)S(1)} %copy.95), kind=kLoop, calls=%fused_computation.5 | loop fusion | flops 16777216 | bytes 9175040 | tf_op jit(solution)/shard_map/convert_element_type | solution.py:126
  340.3 4.4 fusion.51
  344.7 4.4 fusion.52
  349.2 5.2 %add_bitcast_fusion = f32[1,16,64,64,16]{3,2,4,1,0:T(8,128)S(1)} fusion(f32[16,64,16,64]{3,1,2,0:T(8,128)S(1)} %fusion.51, bf16[1,16,1,64,16,16]{3,5,4,2,1,0:T(8,128)(2,1)S(1)} %get-tuple-element.8, s32[16]{0:T(128)S(1)} %get-tuple-element.21), kind=kOutput, calls=%fused_computation.15 | convolution fusion | flops 202389504 | bytes 8912960 | tf_op jit(solution)/shard_map/kx,...ckm->...cxm/dot_general | solution.py:74
  354.4 4.9 subtract_bitcast_fusion
  362.6 58.2 %convert_bitcast_fusion = bf16[1,16,64,64,128]{4,3,2,1,0:T(8,128)(2,1)} fusion(f32[16,64,64,32]{2,1,3,0:T(8,128)S(1)} %maximum_bitcast_fusion, f32[16,128]{1,0:T(8,128)S(1)} %get-tuple-element.28, f32[16,128]{1,0:T(8,128)S(1)} %get-tuple-element.29), kind=kOutput, calls=%fused_computation.6 | convolution fusion | flops 3229622272 | bytes 25182208 | tf_op jit(solution)/shard_map/dot_general | solution.py:78
  420.8 69.6 %all-reduce.2.cloned.1.call-done = bf16[32,16,64,128]{3,2,1,0:T(8,128)(2,1)} async-done(((bf16[32,16,64,128]{3,2,1,0:T(8,128)(2,1)}), bf16[32,16,64,128]{3,2,1,0:T(8,128)(2,1)}) %all-reduce.2.cloned.1.call-update) | async-done | bytes 8388624 | tf_op jit(solution)/shard_map/psum | solution.py:125
  490.4 11.7 %convert_element_type.95 = f32[32,16,64,128]{3,2,1,0:T(8,128)} convert(bf16[32,16,64,128]{3,2,1,0:T(8,128)(2,1)} %all-reduce.2.cloned.1.call-done) | non-fusion elementwise | flops 4194304 | bytes 25165824 | tf_op jit(solution)/shard_map/convert_element_type | solution.py:127
  (61 shorter events, 59.3 us)
Async XLA Ops:
  34.5 42.0 %copy-start = (f32[16,64,64,32]{2,1,0,3:T(8,128)S(1)}, f32[16,64,64,32]{2,1,0,3:T(8,128)}, u32[]{:S(2)}) copy-start(f32[16,64,64,32]{2,1,0,3:T(8,128)} %reshape.397) | copy-start | bytes 25165828
  122.4 121.9 %all-to-all-start = ((bf16[8,2,32768]{2,1,0:T(2,128)(2,1)}), bf16[8,2,32768]{2,1,0:T(2,128)(2,1)S(1)}, u32[]{:S(2)}, u32[]{:S(2)}) async-start(bf16[8,2,32768]{2,1,0:T(2,128)(2,1)} %reshape.424), calls=%async_computation | async-start | bytes 2097152 | tf_op jit(solution)/shard_map/all_to_all | solution.py:119
  157.0 41.9 %copy-start.1 = (f32[16,64,64,32]{2,1,0,3:T(8,128)S(1)}, f32[16,64,64,32]{2,1,0,3:T(8,128)}, u32[]{:S(2)}) copy-start(f32[16,64,64,32]{2,1,0,3:T(8,128)} %reshape.406) | copy-start | bytes 25165828
  244.4 1.0 copy-start.2
  245.3 56.1 %all-to-all-start.2 = ((bf16[8,2,32768]{2,1,0:T(2,128)(2,1)}), bf16[8,2,32768]{2,1,0:T(2,128)(2,1)S(1)}, u32[]{:S(2)}, u32[]{:S(2)}) async-start(bf16[8,2,32768]{2,1,0:T(2,128)(2,1)} %reshape.428), calls=%async_computation.2 | async-start | bytes 2097152 | tf_op jit(solution)/shard_map/all_to_all | solution.py:118
  301.4 34.7 %all-to-all-start.1 = ((bf16[8,2,32768]{2,1,0:T(2,128)(2,1)}), bf16[8,2,32768]{2,1,0:T(2,128)(2,1)}, u32[]{:S(2)}, u32[]{:S(2)}) async-start(bf16[8,2,32768]{2,1,0:T(2,128)(2,1)} %reshape.426), calls=%async_computation.1 | async-start | bytes 2097152 | tf_op jit(solution)/shard_map/all_to_all | solution.py:137
  307.4 183.0 %all-reduce.2.cloned.1.call-start = ((), (), s32[]{:S(2)}) async-start(), calls=%async_computation.3 | async-start | bytes 16777216 | tf_op jit(solution)/shard_map/psum | solution.py:125
Sparse Core Ops, SparseCore 0:
  336.2 154.2 all-reduce.1
where the time goes:
time: 517 us; the launch traced here: 509 us
  matrix products  307 us (59%)
  waiting for transfers between devices  69.6 us (13%)
  local copies, waits for them, and re-layouts  66.4 us (13%)
  other arithmetic  32.5 us (6%)
  starting transfers between devices  19.3 us (4%)
  between operations  14.8 us (3%)
    dot_general x2, matrix products, plane_spectrum(): jnp.einsum('kx,...cxm->...ckm', sin_x, along_z, precision=highest)  83.9 us
    dot_general x2, matrix products, plane_spectrum(): jnp.einsum('kx,...cxm->...ckm', cos_x, along_z, precision=highest)  79.5 us
    psum x1, waiting for transfers between devices, local(): lax.psum(weight_terms(input_modes, cot_modes).astype(jnp.bfloat16), 'batch')  69.6 us
    dot_general x1, matrix products, plane_inverse(): jnp.dot(joined.reshape(-1, 2 * MZ), z_back, precision=highest, preferred_...  58.2 us
    dot_general x2, matrix products, plane_spectrum(): jnp.dot(values.reshape(-1, Z), z_table, preferred_element_type=jnp.float32)  30 us
    unnamed x16, local copies, waits for them, and re-layouts  27.2 us
    another operation x8, local copies, waits for them, and re-layouts  15.9 us
    convert_element_type x1, other arithmetic, local(): weight_terms(input_modes, cot_modes).astype(jnp.bfloat16)  12.6 us
  transfers between devices with their start and end apart: 4, of which 1 were waited for; matrix products, arithmetic and copies ran while one was open for 55% of the time, Pallas kernels for 0%

commit v1 on v0

--- a/solution.py
+++ b/solution.py
@@ -122,8 +122,8 @@
     cot_modes = modes_along_y(moved_cot, cos_y, sin_y)
     input_modes = input_modes.astype(jnp.bfloat16)
     cot_modes = cot_modes.astype(jnp.bfloat16)
-    weight_grad = lax.psum(
-        weight_terms(input_modes, cot_modes).astype(jnp.bfloat16), "batch"
+    weight_grad = jnp.sum(
+        lax.all_gather(weight_terms(input_modes, cot_modes).astype(jnp.bfloat16), "batch"), axis=0
     ).astype(jnp.float32)
     cot_one, cot_two = split_cot(cot_modes)
     grad_real = jnp.einsum(

time: 517 us -> 554 us (1.072)
  waiting for transfers between devices: 69.6 us -> 94.1 us
  other arithmetic: 32.5 us -> 46.5 us
    psum x1 -> x0, waiting for transfers between devices: 69.6 us -> none  [local(): lax.psum(weight_terms(input_modes, cot_modes).astype(jnp.bfloat16), 'batch')]
    all_gather x0 -> x1, waiting for transfers between devices: none -> 60.8 us  [local(): lax.all_gather(weight_terms(input_modes, cot_modes).astype(jnp.bfloat16),...]
    all_to_all x1, waiting for transfers between devices: 0.01 us -> 25.9 us  [local(): lax.all_to_all(plane_modes, 'space', split_axis=1, concat_axis=4, tiled=T...]
    reduce_sum x0 -> x1, other arithmetic: none -> 16.4 us  [local(): jnp.sum(lax.all_gather(weight_terms(input_modes, cot_modes).astype(jnp.bf...]
    all_to_all x1, waiting for transfers between devices: 0.01 us -> 7.47 us  [local(): lax.all_to_all(input_spec, 'space', split_axis=4, concat_axis=1, tiled=True)]
    unnamed x16 -> x14, local copies, waits for them, and re-layouts: 27.2 us -> 24.8 us
  transfers between devices with their start and end apart: 4 -> 4, of which waited for: 1 -> 3; matrix products, arithmetic and copies ran while one was open for 55% -> 44% of each run, Pallas kernels for 0% -> 0%
where the time goes in v1:
time: 554 us; the launch traced here: 546 us
  matrix products  309 us (56%)
  waiting for transfers between devices  94.1 us (17%)
  local copies, waits for them, and re-layouts  64.7 us (12%)
  other arithmetic  46.5 us (8%)
  starting transfers between devices  17.2 us (3%)
  between operations  14.6 us (3%)
    dot_general x2, matrix products, plane_spectrum(): jnp.einsum('kx,...cxm->...ckm', sin_x, along_z, precision=highest)  83.9 us
    dot_general x2, matrix products, plane_spectrum(): jnp.einsum('kx,...cxm->...ckm', cos_x, along_z, precision=highest)  79.7 us
    all_gather x1, waiting for transfers between devices, local(): lax.all_gather(weight_terms(input_modes, cot_modes).astype(jnp.bfloat16),...  60.8 us
    dot_general x1, matrix products, plane_inverse(): jnp.dot(joined.reshape(-1, 2 * MZ), z_back, precision=highest, preferred_...  58.2 us
    dot_general x2, matrix products, plane_spectrum(): jnp.dot(values.reshape(-1, Z), z_table, preferred_element_type=jnp.float32)  30 us
    all_to_all x1, waiting for transfers between devices, local(): lax.all_to_all(plane_modes, 'space', split_axis=1, concat_axis=4, tiled=T...  25.9 us
    unnamed x14, local copies, waits for them, and re-layouts  24.8 us
    another operation x8, local copies, waits for them, and re-layouts  16.5 us
  transfers between devices with their start and end apart: 4, of which 3 were waited for; matrix products, arithmetic and copies ran while one was open for 44% of the time, Pallas kernels for 0%

profile of v1, /device:TPU:0, one launch (start us, length us, event | category | flops | bytes accessed | tf_op | source)
XLA Modules:
  0.0 546.5 jit_solution(2213170119710773648)
XLA Ops:
  7.3 15.0 %convolution_bitcast_fusion.1 = f32[65536,32]{0,1:T(8,128)} fusion(bf16[65536,128]{1,0:T(8,128)(2,1)} %bitcast.209, bf16[128,16]{0,1:T(8,128)(2,1)S(1)} %get-tuple-element.24, bf16[128,16]{0,1:T(8,128)(2,1)S(1)} %get-tuple-element.25), kind=kOutput, calls=%fused_computation.1 | convolution fusion | flops 536887296 | bytes 25174016 | tf_op jit(solution)/shard_map/dot_general | solution.py:30
  22.3 12.2 %reshape.397 = f32[16,64,64,32]{2,1,0,3:T(8,128)} reshape(f32[65536,32]{0,1:T(8,128)} %convolution_bitcast_fusion.1) | data formatting | bytes 16777216 | tf_op jit(solution)/shard_map/reshape
  34.6 41.9 %fusion.15 = f32[1,16,64,16,32]{2,3,4,1,0:T(8,128)S(1)} fusion(f32[16,64,64,32]{2,1,0,3:T(8,128)} %reshape.397, s32[16]{0:T(128)S(1)} %get-tuple-element.21), kind=kOutput, calls=%fused_computation.18 | convolution fusion | flops 402667520 | bytes 10485824 | tf_op jit(solution)/shard_map/kx,...cxm->...ckm/dot_general | solution.py:33
  76.5 39.9 %fusion.12 = f32[1,16,64,16,32]{2,3,4,1,0:T(8,128)S(1)} fusion(f32[16,64,64,32]{2,1,0,3:T(8,128)S(1)} %copy-done, s32[16]{0:T(128)S(1)} %get-tuple-element.21), kind=kOutput, calls=%fused_computation.17 | convolution fusion | flops 402667520 | bytes 10485824 | tf_op jit(solution)/shard_map/kx,...cxm->...ckm/dot_general | solution.py:32
  122.4 7.3 %all-to-all-start = ((bf16[8,2,32768]{2,1,0:T(2,128)(2,1)}), bf16[8,2,32768]{2,1,0:T(2,128)(2,1)S(1)}, u32[]{:S(2)}, u32[]{:S(2)}) async-start(bf16[8,2,32768]{2,1,0:T(2,128)(2,1)} %reshape.425), calls=%async_computation | async-start | bytes 2097152 | tf_op jit(solution)/shard_map/all_to_all | solution.py:119
  129.7 15.0 %convolution_bitcast_fusion = f32[65536,32]{0,1:T(8,128)} fusion(bf16[65536,128]{1,0:T(8,128)(2,1)} %bitcast.210, bf16[128,16]{0,1:T(8,128)(2,1)S(1)} %get-tuple-element.24, bf16[128,16]{0,1:T(8,128)(2,1)S(1)} %get-tuple-element.25), kind=kOutput, calls=%fused_computation | convolution fusion | flops 536887296 | bytes 25174016 | tf_op jit(solution)/shard_map/dot_general | solution.py:30
  144.7 12.2 %reshape.406 = f32[16,64,64,32]{2,1,0,3:T(8,128)} reshape(f32[65536,32]{0,1:T(8,128)} %convolution_bitcast_fusion) | data formatting | bytes 16777216 | tf_op jit(solution)/shard_map/reshape.48
  156.9 41.9 %fusion.21 = f32[1,16,64,16,32]{2,3,4,1,0:T(8,128)S(1)} fusion(f32[16,64,64,32]{2,1,0,3:T(8,128)} %reshape.406, s32[16]{0:T(128)S(1)} %get-tuple-element.21), kind=kOutput, calls=%fused_computation.20 | convolution fusion | flops 402667520 | bytes 10485824 | tf_op jit(solution)/shard_map/kx,...cxm->...ckm/dot_general | solution.py:33
  198.9 39.8 %fusion.18 = f32[1,16,64,16,32]{2,3,4,1,0:T(8,128)S(1)} fusion(f32[16,64,64,32]{2,1,0,3:T(8,128)S(1)} %copy-done.1, s32[16]{0:T(128)S(1)} %get-tuple-element.21), kind=kOutput, calls=%fused_computation.19 | convolution fusion | flops 402667520 | bytes 10485824 | tf_op jit(solution)/shard_map/kx,...cxm->...ckm/dot_general | solution.py:32
  244.5 6.0 %all-to-all-start.2 = ((bf16[8,2,32768]{2,1,0:T(2,128)(2,1)}), bf16[8,2,32768]{2,1,0:T(2,128)(2,1)}, u32[]{:S(2)}, u32[]{:S(2)}) async-start(bf16[8,2,32768]{2,1,0:T(2,128)(2,1)} %reshape.429), calls=%async_computation.2 | async-start | bytes 2097152 | tf_op jit(solution)/shard_map/all_to_all | solution.py:118
  268.6 7.5 %all-to-all-done.2 = bf16[8,2,32768]{2,1,0:T(2,128)(2,1)} async-done(((bf16[8,2,32768]{2,1,0:T(2,128)(2,1)}), bf16[8,2,32768]{2,1,0:T(2,128)(2,1)}, u32[]{:S(2)}, u32[]{:S(2)}) %all-to-all-start.2) | async-done | bytes 1048608 | tf_op jit(solution)/shard_map/all_to_all | solution.py:118
  298.8 12.0 %add_convert_fusion = bf16[32,16,64,128]{3,2,1,0:T(8,128)(2,1)} fusion(f32[32,16,128]{2,1,0:T(8,128)S(1)} %get-tuple-element.19, f32[32,16,64]{2,1,0:T(8,128)S(1)} %copy.96, f32[32,16,128]{2,1,0:T(8,128)S(1)} %get-tuple-element.14, f32[32,16,64]{2,1,0:T(8,128)S(1)} %copy.95), kind=kLoop, calls=%fused_computation.5 | loop fusion | flops 16777216 | bytes 9175040 | tf_op jit(solution)/shard_map/convert_element_type | solution.py:126
  310.8 7.8 %fusion.64 = f32[32,16,1,64]{3,2,1,0:T(1,128)S(1)} fusion(bf16[32,16,64,128]{3,2,1,0:T(8,128)(2,1)} %param.5, bf16[32,16,128,1]{2,1,0,3:T(8,128)(2,1)S(1)} %get-tuple-element.15), kind=kOutput, calls=%fused_computation.76 | convolution fusion | flops 8388608 | bytes 8650752 | tf_op jit(solution)/shard_map/pbkj,pkij->pbki/dot_general | solution.py:129
  319.4 9.9 %fusion.62 = f32[32,16,1,64]{3,2,1,0:T(1,128)S(1)} fusion(bf16[32,16,64,128]{3,2,1,0:T(8,128)(2,1)} %param.5, bf16[32,16,128,1]{2,1,0,3:T(8,128)(2,1)S(1)} %get-tuple-element.18), kind=kOutput, calls=%fused_computation.74 | convolution fusion | flops 8388608 | bytes 8650752 | tf_op jit(solution)/shard_map/pbkj,pkij->pbki/dot_general | solution.py:132
  337.6 3.8 all-to-all-start.1
  341.4 25.9 %all-to-all-done.1 = bf16[8,2,32768]{2,1,0:T(2,128)(2,1)S(1)} async-done(((bf16[8,2,32768]{2,1,0:T(2,128)(2,1)}), bf16[8,2,32768]{2,1,0:T(2,128)(2,1)S(1)}, u32[]{:S(2)}, u32[]{:S(2)}) %all-to-all-start.1) | async-done | bytes 1048608 | tf_op jit(solution)/shard_map/all_to_all | solution.py:137
  370.0 4.4 fusion.51
  374.5 4.4 fusion.52
  378.9 5.1 add_bitcast_fusion
  384.1 4.9 subtract_bitcast_fusion
  392.4 58.2 %convert_bitcast_fusion = bf16[1,16,64,64,128]{4,3,2,1,0:T(8,128)(2,1)} fusion(f32[16,64,64,32]{2,1,3,0:T(8,128)S(1)} %maximum_bitcast_fusion, f32[16,128]{1,0:T(8,128)S(1)} %get-tuple-element.28, f32[16,128]{1,0:T(8,128)S(1)} %get-tuple-element.29), kind=kOutput, calls=%fused_computation.6 | convolution fusion | flops 3229622272 | bytes 25182208 | tf_op jit(solution)/shard_map/dot_general | solution.py:78
  450.5 60.8 %all-gather.3.cloned.1.call-done = bf16[128,16,64,128]{3,2,1,0:T(8,128)(2,1)} async-done(((bf16[32,16,64,128]{3,2,1,0:T(8,128)(2,1)}), bf16[128,16,64,128]{3,2,1,0:T(8,128)(2,1)}) %all-gather.3.cloned.1.call-update) | async-done | bytes 33554448 | tf_op jit(solution)/shard_map/all_gather | solution.py:126
  511.3 16.4 %reduce_sum.12 = bf16[32,16,64,128]{3,2,1,0:T(8,128)(2,1)} reduce(bf16[4,32,16,64,128]{4,3,2,1,0:T(8,128)(2,1)} %bitcast.211, bf16[]{:T(256)} %constant.55.clone.1), dimensions={0}, to_apply=%region_0.1 | reduce | flops 12582912 | bytes 41943040 | tf_op jit(solution)/shard_map/reduce_sum | solution.py:125
  527.7 11.7 %convert_element_type.97 = f32[32,16,64,128]{3,2,1,0:T(8,128)} convert(bf16[32,16,64,128]{3,2,1,0:T(8,128)(2,1)} %reduce_sum.12) | non-fusion elementwise | flops 4194304 | bytes 25165824 | tf_op jit(solution)/shard_map/convert_element_type | solution.py:127
  (60 shorter events, 67.8 us)
Async XLA Ops:
  34.6 42.0 %copy-start = (f32[16,64,64,32]{2,1,0,3:T(8,128)S(1)}, f32[16,64,64,32]{2,1,0,3:T(8,128)}, u32[]{:S(2)}) copy-start(f32[16,64,64,32]{2,1,0,3:T(8,128)} %reshape.397) | copy-start | bytes 25165828
  122.4 122.1 %all-to-all-start = ((bf16[8,2,32768]{2,1,0:T(2,128)(2,1)}), bf16[8,2,32768]{2,1,0:T(2,128)(2,1)S(1)}, u32[]{:S(2)}, u32[]{:S(2)}) async-start(bf16[8,2,32768]{2,1,0:T(2,128)(2,1)} %reshape.425), calls=%async_computation | async-start | bytes 2097152 | tf_op jit(solution)/shard_map/all_to_all | solution.py:119
  156.9 41.9 %copy-start.1 = (f32[16,64,64,32]{2,1,0,3:T(8,128)S(1)}, f32[16,64,64,32]{2,1,0,3:T(8,128)}, u32[]{:S(2)}) copy-start(f32[16,64,64,32]{2,1,0,3:T(8,128)} %reshape.406) | copy-start | bytes 25165828
  244.5 31.5 %all-to-all-start.2 = ((bf16[8,2,32768]{2,1,0:T(2,128)(2,1)}), bf16[8,2,32768]{2,1,0:T(2,128)(2,1)}, u32[]{:S(2)}, u32[]{:S(2)}) async-start(bf16[8,2,32768]{2,1,0:T(2,128)(2,1)} %reshape.429), calls=%async_computation.2 | async-start | bytes 2097152 | tf_op jit(solution)/shard_map/all_to_all | solution.py:118
  250.5 260.7 %all-gather.3.cloned.1.call-start = ((), (), s32[]{:S(2)}) async-start(), calls=%async_computation.3 | async-start | bytes 41943040 | tf_op jit(solution)/shard_map/all_gather | solution.py:126
  337.6 29.8 %all-to-all-start.1 = ((bf16[8,2,32768]{2,1,0:T(2,128)(2,1)}), bf16[8,2,32768]{2,1,0:T(2,128)(2,1)S(1)}, u32[]{:S(2)}, u32[]{:S(2)}) async-start(bf16[8,2,32768]{2,1,0:T(2,128)(2,1)} %reshape.427), calls=%async_computation.1 | async-start | bytes 2097152 | tf_op jit(solution)/shard_map/all_to_all | solution.py:137
Sparse Core Ops, SparseCore 0:
  310.9 200.2 all-gather.2
